TPU v7x, 32 devices: a whole 2x2x4 slice. The times are simulated.
32 devices in a mesh: row: 8 (over z, x), col: 4 (over y, core).
Axes of the slice: x: 2, y: 2, z: 4, core: 2. Of those that a mesh axis runs over, the one named last changes fastest.
Arguments:
- basis_blocks: float32 [8, 16, 262144], P(None, None, ('col', 'row')), may hold values from -6 to 6
- tile_values: bfloat16 [4, 8, 384, 128, 128], P('col', 'row'), may hold values from -0.375 to 0.375
- tile_rows: int32 [4, 8, 384], P('col', 'row'), may hold values from 0 to 511
- tile_column: int32 [4, 8, 384], P('col', 'row'), may hold values from 0 to 255
- tile_count: int32 [4, 8], P('col', 'row'), may hold values from 1 to 384, as said below
- diagonal: float32 [262144], P(('col', 'row')), may hold values from 1 to 6
Outputs:
- new_block: float32 [16, 262144], P(None, ('col', 'row'))
- coefficients: float32 [8, 16, 16], replicated
- triangle: float32 [16, 16], replicated
Inputs may be any that keep to these rules, and one draw needn't show every extreme that they name: Each operator block stores tile_count tiles in its first slots; at most 384, and some block has exactly 384 in every draw. Slots past the count hold arbitrary data and are ignored.
All inputs are finite; a program needn't handle non-finite values.
Results may differ from a plain program's by a relative error of at most 0.0031.
Values may be sent and summed in bfloat16 or wider, within the bound.
A program may use at most 128 MiB of HBM per device.

v0:
```python
import jax
import jax.numpy as jnp
from jax import lax
from jax.sharding import PartitionSpec as P


def local(basis_blocks, tile_values, tile_rows, tile_column, tile_count, diagonal):
    rhs_width = basis_blocks.shape[1]
    seg_rows = basis_blocks.shape[2]
    total_rows = seg_rows * lax.axis_size("row") * lax.axis_size("col")
    block_tiles = lax.axis_size("row") * seg_rows // 128
    vector = basis_blocks[-1].astype(jnp.bfloat16)
    expanded = lax.all_gather(vector, "col", axis=1, tiled=True)
    xblocks = expanded.reshape(rhs_width, -1, 128)
    values = tile_values[0, 0]
    row_ids = tile_rows[0, 0]
    column_ids = tile_column[0, 0]
    live_count = tile_count[0, 0]
    live_tiles = jnp.arange(values.shape[0], dtype=jnp.int32) < live_count
    gathered = jnp.take(xblocks, column_ids, axis=1)
    products = jnp.einsum("stj,tji->tsi", gathered, values, preferred_element_type=jnp.float32)
    inside = live_tiles & (row_ids >= 0) & (row_ids < 0 + block_tiles)
    segment_ids = jnp.where(inside, row_ids - 0, block_tiles)
    summed = jax.ops.segment_sum(products, segment_ids, num_segments=block_tiles + 1)
    folded = lax.psum_scatter(summed[:block_tiles], "row", scatter_dimension=0, tiled=True)
    image_rows = folded.transpose(1, 0, 2).reshape(rhs_width, seg_rows)
    image_rows = image_rows + diagonal[None, :] * basis_blocks[-1]
    highest = lax.Precision.HIGHEST
    local_proj = jnp.einsum("kap,bp->kab", basis_blocks, image_rows, precision=highest)
    local_self = jnp.dot(image_rows, image_rows.T, precision=highest)
    local_basis = jnp.einsum("kap,lcp->kalc", basis_blocks, basis_blocks, precision=highest)
    proj_sum, image_sum, basis_sum = lax.psum((local_proj, local_self, local_basis), ("row", "col"))
    coefficients = proj_sum / total_rows
    image_gram = image_sum / total_rows
    basis_gram = basis_sum / total_rows
    projected = image_rows - jnp.einsum(
        "kab,kap->bp", coefficients, basis_blocks, precision=highest
    )
    cross_term = jnp.einsum("kab,kad->bd", coefficients, coefficients, precision=highest)
    basis_term = jnp.einsum(
        "kab,kalc,lcd->bd", coefficients, basis_gram, coefficients, precision=highest
    )
    gram_matrix = image_gram - 2.0 * cross_term + basis_term
    lower_factor = jnp.linalg.cholesky(gram_matrix)
    new_block = lax.linalg.triangular_solve(lower_factor, projected, left_side=True, lower=True)
    return (new_block, coefficients, lower_factor.T)


def solution(mesh):
    in_specs = (
        P(None, None, ("col", "row")),
        P("col", "row", None, None, None),
        P("col", "row", None),
        P("col", "row", None),
        P("col", "row"),
        P(("col", "row")),
    )
    out_specs = (P(None, ("col", "row")), P(), P())
    return jax.shard_map(local, mesh=mesh, in_specs=in_specs, out_specs=out_specs, check_vma=False)
```

profile of v0, /device:TPU:0, one launch (start us, length us, event | category | flops | bytes accessed | tf_op | source)
XLA Modules:
  0.0 285.5 jit_solution(4340497072909810050)
XLA Ops:
  8.0 1.8 bitcast_convert_fusion
  10.5 0.7 reduce.7
  11.2 0.7 fusion.22
  11.9 0.7 fusion.23
  12.7 17.7 %all-gather.2.cloned.1.call-done = bf16[16,32768]{1,0:T(8,128)(2,1)} async-done(((bf16[16,8192]{1,0:T(8,128)(2,1)}), bf16[16,32768]{1,0:T(8,128)(2,1)}) %all-gather.2.cloned.1.call-update) | async-done | bytes 1048592 | tf_op jit(solution)/shard_map/all_gather | solution.py:13
  30.4 1.4 copy_bitcast_fusion
  31.8 2.6 gather_fusion
  34.4 6.9 %fusion = f32[384,16,128]{2,1,0:T(8,128)S(1)} fusion(bf16[1,1,384,128,128]{4,3,2,1,0:T(8,128)(2,1)} %param.7, bf16[384,16,128]{2,1,0:T(8,128)(2,1)} %gather_fusion, pred[384]{0:T(512)(128)(4,1)S(1)} %compare_and_fusion), kind=kOutput, calls=%fused_computation.2 | convolution fusion | flops 202113024 | bytes 17301888 | tf_op jit(solution)/shard_map/stj,tji->tsi/dot_general | solution.py:21
  41.2 2.2 broadcast_in_dim.19
  43.5 51.1 %scatter_fusion = f32[513,16,128]{2,1,0:T(8,128)} fusion(f32[513,16,128]{2,1,0:T(8,128)} %broadcast_in_dim.19, s32[384]{0:T(512)S(1)} %fusion.23, f32[384,16,128]{2,1,0:T(8,128)S(1)} %fusion), kind=kCustom, calls=%fused_computation.1 | custom fusion | flops 786432 | bytes 9438720 | tf_op jit(solution)/shard_map/scatter-add | solution.py:24
  94.6 4.4 %slice.21 = f32[512,16,128]{2,1,0:T(8,128)} slice(f32[513,16,128]{2,1,0:T(8,128)} %scatter_fusion), slice={[0:512], [0:16], [0:128]} | slice | bytes 8388608 | tf_op jit(solution)/shard_map/slice | solution.py:25
  99.3 18.0 %fusion.3 = f32[8,16,8,16]{3,1,2,0:T(8,128)} fusion(f32[8,16,8192]{2,1,0:T(8,128)} %param.6), kind=kOutput, calls=%fused_computation.6 | convolution fusion | flops 1610612736 | bytes 4259840 | tf_op jit(solution)/shard_map/kap,lcp->kalc/dot_general | solution.py:31
  117.3 1.1 slice_bitcast_fusion
  118.5 70.4 %reduce-scatter.2.cloned.1.call-done = f32[64,16,128]{2,1,0:T(8,128)} async-done(((f32[512,16,128]{2,1,0:T(8,128)}), f32[64,16,128]{2,1,0:T(8,128)}) %reduce-scatter.2.cloned.1.call-update) | async-done | bytes 524304 | tf_op jit(solution)/shard_map/reduce_scatter | solution.py:25
  188.9 17.2 %convolution_bitcast_fusion.1 = f32[8,16,16]{1,2,0:T(8,128)S(1)} fusion(f32[8,16,8192]{2,1,0:T(8,128)} %param.6, f32[8192]{0:T(1024)S(1)} %copy-done.1, f32[64,16,128]{2,1,0:T(8,128)} %reduce-scatter.2.cloned.1.call-done), kind=kOutput, calls=%fused_computation.12 | convolution fusion | flops 201588736 | bytes 5283840 | tf_op jit(solution)/shard_map/kap,bp->kab/dot_general | solution.py:29
  206.1 1.0 convolution_bitcast_fusion.5
  207.1 41.0 %all-reduce = (f32[8,16,16]{1,2,0:T(8,128)S(1)}, f32[16,16]{0,1:T(8,128)S(1)}) all-reduce(f32[8,16,16]{1,2,0:T(8,128)S(1)} %convolution_bitcast_fusion.1, f32[16,16]{0,1:T(8,128)S(1)} %convolution_bitcast_fusion.5), channel_id=1, replica_groups=mesh['row'=8,'col'=4] {'row','col'}, use_global_device_ids=true, to_apply=%region_3.4 | all-reduce | flops 2304 | bytes 18432 | tf_op jit(solution)/shard_map/psum | solution.py:32
  248.1 14.4 %all-reduce.3.cloned.1.call-done = f32[8,16,8,16]{3,1,2,0:T(8,128)} async-done(((f32[8,16,8,16]{3,1,2,0:T(8,128)}), f32[8,16,8,16]{3,1,2,0:T(8,128)}) %all-reduce.3.cloned.1.call-update) | async-done | bytes 65552 | tf_op jit(solution)/shard_map/psum | solution.py:32
  262.5 1.4 convolution_bitcast_fusion.2
  264.4 1.5 cholesky.16
  267.2 1.2 custom-call.6
  269.1 0.7 copy.41
  269.9 6.7 %fusion.2 = f32[16,8192]{1,0:T(8,128)S(1)} fusion(f32[8,16,8192]{2,1,0:T(8,128)} %param.6, f32[8192]{0:T(1024)S(1)} %copy-done.1, f32[8,16,16]{1,2,0:T(8,128)S(1)} %get-tuple-element.12, f32[64,16,128]{2,1,0:T(8,128)S(1)} %copy-done), kind=kOutput, calls=%fused_computation.5 | convolution fusion | flops 201721856 | bytes 5808128 | tf_op jit(solution)/shard_map/kab,kap->bp/dot_general | solution.py:36
  276.6 1.4 fusion.18
  (22 shorter events, 3.0 us)
Async XLA Ops:
  8.0 22.4 %all-gather.2.cloned.1.call-start = ((), (), s32[]{:S(2)}) async-start(), calls=%async_computation.1 | async-start | bytes 1310720 | tf_op jit(solution)/shard_map/all_gather | solution.py:13
  9.8 179.0 %reduce-scatter.2.cloned.1.call-start = ((), (), s32[]{:S(2)}) async-start(), calls=%async_computation.2 | async-start | bytes 4718592 | tf_op jit(solution)/shard_map/reduce_scatter | solution.py:25
  99.0 89.8 %copy-start.1 = (f32[8192]{0:T(1024)S(1)}, f32[8192]{0:T(1024)}, u32[]{:S(2)}) copy-start(f32[8192]{0:T(1024)} %param.11) | copy-start | bytes 98308
  99.0 163.4 %all-reduce.3.cloned.1.call-start = ((), (), s32[]{:S(2)}) async-start(), calls=%async_computation.3 | async-start | bytes 1048576 | tf_op jit(solution)/shard_map/psum | solution.py:32
  188.9 17.2 %copy-start = (f32[64,16,128]{2,1,0:T(8,128)S(1)}, f32[64,16,128]{2,1,0:T(8,128)}, u32[]{:S(2)}) copy-start(f32[64,16,128]{2,1,0:T(8,128)} %reduce-scatter.2.cloned.1.call-done) | copy-start | bytes 1572868
Sparse Core Ops, SparseCore 0:
  10.9 19.4 all-gather.1
  99.1 89.6 reduce-scatter.1
Sparse Core Ops, SparseCore 1:
  117.4 145.0 all-reduce.2
where the time goes:
time: 288 us; the launch traced here: 285 us
  waiting for transfers between devices  103 us (36%)
  other arithmetic  57.3 us (20%)
  matrix products  53.1 us (18%)
  blocking collectives  41 us (14%)
  between operations  16.2 us (6%)
  local copies, waits for them, and re-layouts  15.1 us (5%)
    reduce_scatter x1, waiting for transfers between devices, local(): lax.psum_scatter(summed[:block_tiles], 'row', scatter_dimension=0, tiled=...  70.4 us
    scatter-add x1, other arithmetic, local(): jax.ops.segment_sum(products, segment_ids, num_segments=block_tiles + 1)  51.1 us
    psum x1, blocking collectives, local(): lax.psum((local_proj, local_self, local_basis), ('row', 'col'))  41 us
    dot_general x1, matrix products, local(): jnp.einsum('kap,lcp->kalc', basis_blocks, basis_blocks, precision=highest)  18 us
    all_gather x1, waiting for transfers between devices, local(): expanded = lax.all_gather(vector, 'col', axis=1, tiled=True)  17.7 us
    dot_general x1, matrix products, local(): jnp.einsum('kap,bp->kab', basis_blocks, image_rows, precision=highest)  17.2 us
    psum x1, waiting for transfers between devices, local(): lax.psum((local_proj, local_self, local_basis), ('row', 'col'))  14.4 us
    dot_general x1, matrix products, local(): jnp.einsum('stj,tji->tsi', gathered, values, preferred_element_type=jnp.f...  6.87 us
  transfers between devices with their start and end apart: 3, of which 3 were waited for; matrix products, arithmetic and copies ran while one was open for 14% of the time, Pallas kernels for 0%

commit v1 on v0

--- a/solution.py
+++ b/solution.py
@@ -10,7 +10,12 @@
     total_rows = seg_rows * lax.axis_size("row") * lax.axis_size("col")
     block_tiles = lax.axis_size("row") * seg_rows // 128
     vector = basis_blocks[-1].astype(jnp.bfloat16)
-    expanded = lax.all_gather(vector, "col", axis=1, tiled=True)
+    ring = [vector]
+    for hop in range(3):
+        ring.append(lax.ppermute(ring[-1], "col", [(dev, (dev + 1) % 4) for dev in range(4)]))
+    expanded = jnp.roll(
+        jnp.concatenate(ring[::-1], axis=1), (lax.axis_index("col") + 1) * ring[0].shape[1], axis=1
+    )
     xblocks = expanded.reshape(rhs_width, -1, 128)
     values = tile_values[0, 0]
     row_ids = tile_rows[0, 0]

time: 288 us -> 286 us (level)
  waiting for transfers between devices: 103 us -> 100 us
    all_gather x1 -> x0, waiting for transfers between devices: 17.7 us -> none  [local(): expanded = lax.all_gather(vector, 'col', axis=1, tiled=True)]
    ppermute x0 -> x3, waiting for transfers between devices: none -> 14.8 us  [local(): lax.ppermute(ring[-1], 'col', [(dev, (dev + 1) % 4) for dev in range(4)])]
  transfers between devices with their start and end apart: 3 -> 5, of which waited for: 3 -> 5; matrix products, arithmetic and copies ran while one was open for 14% -> 14% of each run, Pallas kernels for 0% -> 0%
where the time goes in v1:
time: 286 us; the launch traced here: 284 us
  waiting for transfers between devices  100 us (35%)
  other arithmetic  57.3 us (20%)
  matrix products  53.1 us (19%)
  blocking collectives  40.9 us (14%)
  between operations  16.3 us (6%)
  local copies, waits for them, and re-layouts  15.4 us (5%)
    reduce_scatter x1, waiting for transfers between devices, local(): lax.psum_scatter(summed[:block_tiles], 'row', scatter_dimension=0, tiled=...  70.4 us
    scatter-add x1, other arithmetic, local(): jax.ops.segment_sum(products, segment_ids, num_segments=block_tiles + 1)  51.1 us
    psum x1, blocking collectives, local(): lax.psum((local_proj, local_self, local_basis), ('row', 'col'))  40.9 us
    dot_general x1, matrix products, local(): jnp.einsum('kap,lcp->kalc', basis_blocks, basis_blocks, precision=highest)  18 us
    dot_general x1, matrix products, local(): jnp.einsum('kap,bp->kab', basis_blocks, image_rows, precision=highest)  17.2 us
    psum x1, waiting for transfers between devices, local(): lax.psum((local_proj, local_self, local_basis), ('row', 'col'))  15 us
    ppermute x3, waiting for transfers between devices, local(): lax.ppermute(ring[-1], 'col', [(dev, (dev + 1) % 4) for dev in range(4)])  14.8 us
    dot_general x1, matrix products, local(): jnp.einsum('stj,tji->tsi', gathered, values, preferred_element_type=jnp.f...  6.87 us
  transfers between devices with their start and end apart: 5, of which 5 were waited for; matrix products, arithmetic and copies ran while one was open for 14% of the time, Pallas kernels for 0%

profile of v1, /device:TPU:0, one launch (start us, length us, event | category | flops | bytes accessed | tf_op | source)
XLA Modules:
  0.0 283.9 jit_solution(3104047999241812338)
XLA Ops:
  8.0 1.1 bitcast_convert_fusion
  9.7 6.0 %collective-permute-done = bf16[16,8192]{1,0:T(8,128)(2,1)S(1)} collective-permute-done((bf16[16,8192]{1,0:T(8,128)(2,1)S(1)}, bf16[16,8192]{1,0:T(8,128)(2,1)S(1)}, u32[]{:S(2)}, u32[]{:S(2)}) %collective-permute-start) | collective-permute-done | bytes 262176 | tf_op jit(solution)/shard_map/ppermute | solution.py:15
  17.7 3.7 %collective-permute-done.1 = bf16[16,8192]{1,0:T(8,128)(2,1)S(1)} collective-permute-done((bf16[16,8192]{1,0:T(8,128)(2,1)S(1)}, bf16[16,8192]{1,0:T(8,128)(2,1)S(1)}, u32[]{:S(2)}, u32[]{:S(2)}) %collective-permute-start.1) | collective-permute-done | bytes 262176 | tf_op jit(solution)/shard_map/ppermute | solution.py:15
  22.2 5.0 %collective-permute-done.2 = bf16[16,8192]{1,0:T(8,128)(2,1)S(1)} collective-permute-done((bf16[16,8192]{1,0:T(8,128)(2,1)S(1)}, bf16[16,8192]{1,0:T(8,128)(2,1)S(1)}, u32[]{:S(2)}, u32[]{:S(2)}) %collective-permute-start.2) | collective-permute-done | bytes 262176 | tf_op jit(solution)/shard_map/ppermute | solution.py:15
  27.3 1.1 constant_dynamic-update-slice_fusion.4
  28.5 1.1 constant_dynamic-update-slice_fusion
  29.8 2.6 gather_fusion
  32.3 6.9 %fusion = f32[384,16,128]{2,1,0:T(8,128)S(1)} fusion(bf16[1,1,384,128,128]{4,3,2,1,0:T(8,128)(2,1)} %param.7, bf16[384,16,128]{2,1,0:T(8,128)(2,1)} %gather_fusion, pred[384]{0:T(512)(128)(4,1)S(1)} %compare_and_fusion), kind=kOutput, calls=%fused_computation.2 | convolution fusion | flops 202113024 | bytes 17301888 | tf_op jit(solution)/shard_map/stj,tji->tsi/dot_general | solution.py:26
  39.2 2.2 broadcast_in_dim.19
  41.4 51.1 %scatter_fusion = f32[513,16,128]{2,1,0:T(8,128)} fusion(f32[513,16,128]{2,1,0:T(8,128)} %broadcast_in_dim.19, s32[384]{0:T(512)S(1)} %fusion.23, f32[384,16,128]{2,1,0:T(8,128)S(1)} %fusion), kind=kCustom, calls=%fused_computation.1 | custom fusion | flops 786432 | bytes 9438720 | tf_op jit(solution)/shard_map/scatter-add | solution.py:29
  92.5 4.4 %slice.21 = f32[512,16,128]{2,1,0:T(8,128)} slice(f32[513,16,128]{2,1,0:T(8,128)} %scatter_fusion), slice={[0:512], [0:16], [0:128]} | slice | bytes 8388608 | tf_op jit(solution)/shard_map/slice | solution.py:30
  97.2 18.0 %fusion.3 = f32[8,16,8,16]{3,1,2,0:T(8,128)} fusion(f32[8,16,8192]{2,1,0:T(8,128)} %param.6), kind=kOutput, calls=%fused_computation.6 | convolution fusion | flops 1610612736 | bytes 4259840 | tf_op jit(solution)/shard_map/kap,lcp->kalc/dot_general | solution.py:36
  115.2 1.1 slice_bitcast_fusion
  116.4 70.4 %reduce-scatter.2.cloned.1.call-done = f32[64,16,128]{2,1,0:T(8,128)} async-done(((f32[512,16,128]{2,1,0:T(8,128)}), f32[64,16,128]{2,1,0:T(8,128)}) %reduce-scatter.2.cloned.1.call-update) | async-done | bytes 524304 | tf_op jit(solution)/shard_map/reduce_scatter | solution.py:30
  186.8 17.2 %convolution_bitcast_fusion.1 = f32[8,16,16]{1,2,0:T(8,128)S(1)} fusion(f32[8,16,8192]{2,1,0:T(8,128)} %param.6, f32[8192]{0:T(1024)S(1)} %copy-done.1, f32[64,16,128]{2,1,0:T(8,128)} %reduce-scatter.2.cloned.1.call-done), kind=kOutput, calls=%fused_computation.12 | convolution fusion | flops 201588736 | bytes 5283840 | tf_op jit(solution)/shard_map/kap,bp->kab/dot_general | solution.py:34
  204.1 1.0 convolution_bitcast_fusion.5
  205.1 40.9 %all-reduce = (f32[8,16,16]{1,2,0:T(8,128)S(1)}, f32[16,16]{0,1:T(8,128)S(1)}) all-reduce(f32[8,16,16]{1,2,0:T(8,128)S(1)} %convolution_bitcast_fusion.1, f32[16,16]{0,1:T(8,128)S(1)} %convolution_bitcast_fusion.5), channel_id=1, replica_groups=mesh['row'=8,'col'=4] {'row','col'}, use_global_device_ids=true, to_apply=%region_3.4 | all-reduce | flops 2304 | bytes 18432 | tf_op jit(solution)/shard_map/psum | solution.py:37
  246.0 15.0 %all-reduce.3.cloned.1.call-done = f32[8,16,8,16]{3,1,2,0:T(8,128)} async-done(((f32[8,16,8,16]{3,1,2,0:T(8,128)}), f32[8,16,8,16]{3,1,2,0:T(8,128)}) %all-reduce.3.cloned.1.call-update) | async-done | bytes 65552 | tf_op jit(solution)/shard_map/psum | solution.py:37
  260.9 1.4 convolution_bitcast_fusion.2
  262.9 1.5 cholesky.16
  265.7 1.2 custom-call.6
  267.6 0.7 copy.41
  268.3 6.7 %fusion.2 = f32[16,8192]{1,0:T(8,128)S(1)} fusion(f32[8,16,8192]{2,1,0:T(8,128)} %param.6, f32[8192]{0:T(1024)S(1)} %copy-done.1, f32[8,16,16]{1,2,0:T(8,128)S(1)} %get-tuple-element.12, f32[64,16,128]{2,1,0:T(8,128)S(1)} %copy-done), kind=kOutput, calls=%fused_computation.5 | convolution fusion | flops 201721856 | bytes 5808128 | tf_op jit(solution)/shard_map/kab,kap->bp/dot_general | solution.py:41
  275.1 1.4 fusion.18
  (33 shorter events, 5.9 us)
Async XLA Ops:
  8.0 178.8 %reduce-scatter.2.cloned.1.call-start = ((), (), s32[]{:S(2)}) async-start(), calls=%async_computation.1 | async-start | bytes 4718592 | tf_op jit(solution)/shard_map/reduce_scatter | solution.py:30
  9.1 6.5 %collective-permute-start = (bf16[16,8192]{1,0:T(8,128)(2,1)S(1)}, bf16[16,8192]{1,0:T(8,128)(2,1)S(1)}, u32[]{:S(2)}, u32[]{:S(2)}) collective-permute-start(bf16[16,8192]{1,0:T(8,128)(2,1)S(1)} %bitcast_convert_fusion), channel_id=1, source_target_pairs={{0,1},{1,2},{2,3},{3,0},{4,5},{5,6},{6,7},{7,4},{8,9},{9,10},{10,1... | collective-permute-start | bytes 786440 | tf_op jit(solution)/shard_map/ppermute | solution.py:15
  15.7 5.8 %collective-permute-start.1 = (bf16[16,8192]{1,0:T(8,128)(2,1)S(1)}, bf16[16,8192]{1,0:T(8,128)(2,1)S(1)}, u32[]{:S(2)}, u32[]{:S(2)}) collective-permute-start(bf16[16,8192]{1,0:T(8,128)(2,1)S(1)} %collective-permute-done), channel_id=1, source_target_pairs={{0,1},{1,2},{2,3},{3,0},{4,5},{5,6},{6,7},{7,4},{8,9},{9,10},{10,1... | collective-permute-start | bytes 786440 | tf_op jit(solution)/shard_map/ppermute | solution.py:15
  21.5 5.8 %collective-permute-start.2 = (bf16[16,8192]{1,0:T(8,128)(2,1)S(1)}, bf16[16,8192]{1,0:T(8,128)(2,1)S(1)}, u32[]{:S(2)}, u32[]{:S(2)}) collective-permute-start(bf16[16,8192]{1,0:T(8,128)(2,1)S(1)} %collective-permute-done.1), channel_id=1, source_target_pairs={{0,1},{1,2},{2,3},{3,0},{4,5},{5,6},{6,7},{7,4},{8,9},{9,10},{10,1... | collective-permute-start | bytes 786440 | tf_op jit(solution)/shard_map/ppermute | solution.py:15
  97.0 164.0 %all-reduce.3.cloned.1.call-start = ((), (), s32[]{:S(2)}) async-start(), calls=%async_computation.2 | async-start | bytes 1048576 | tf_op jit(solution)/shard_map/psum | solution.py:37
  115.2 71.6 %copy-start.1 = (f32[8192]{0:T(1024)S(1)}, f32[8192]{0:T(1024)}, u32[]{:S(2)}) copy-start(f32[8192]{0:T(1024)} %param.11) | copy-start | bytes 98308
  186.8 17.2 %copy-start = (f32[64,16,128]{2,1,0:T(8,128)S(1)}, f32[64,16,128]{2,1,0:T(8,128)}, u32[]{:S(2)}) copy-start(f32[64,16,128]{2,1,0:T(8,128)} %reduce-scatter.2.cloned.1.call-done) | copy-start | bytes 1572868
Sparse Core Ops, SparseCore 0:
  97.1 89.6 reduce-scatter.1
Sparse Core Ops, SparseCore 1:
  115.3 145.6 all-reduce.2
